TPU v7x, 256 devices: a whole 4x4x8 slice. The times are simulated.
256 devices in a mesh: row: 8 (over x, core), col: 32 (over z, y).
Axes of the slice: x: 4, y: 4, z: 8, core: 2. Of those that a mesh axis runs over, the one named last changes fastest.
Arguments:
- trailing: float32 [16384, 16384], P('row', 'col'), may hold values from -9 to 9
- panel: float32 [16384, 256], P('row'), may hold values from -21 to 21
Outputs:
- updated: float32 [16384, 16384], P('row', 'col')
- band: float32 [256, 256], replicated
All inputs are finite; a program needn't handle non-finite values.
Results may differ from a plain program's by a relative error of at most 0.0003.
Values sent between devices are 32-bit elements; how exact they have to be, the bound alone decides.
No kernel may reach another device: no remote copies, remote signals or barrier semaphores. Data moves between devices by JAX's collectives and lax.ppermute only.
A program may use at most 128 MiB of HBM per device.

v0:
```python
import jax
import jax.numpy as jnp
from jax import lax
from jax.sharding import Mesh
from jax.sharding import PartitionSpec as P

COL = ("col_0", "col_1")


def copy_for_each(x, axis):
    devices = lax.axis_size(axis)
    return lax.all_to_all(jnp.broadcast_to(x[None], (devices, *x.shape)), axis, 0, 0, tiled=True)


def of_everyone(x, axis):
    everything = copy_for_each(x, axis)
    return jnp.sum(everything, axis=0)


def broadcast(x, axis, root):
    return lax.dynamic_index_in_dim(lax.all_gather(x, axis), root, 0, keepdims=False)


def padded_to(lines, devices):
    spare = -lines.shape[0] % devices
    if not spare:
        return lines
    return jnp.concatenate([lines, jnp.zeros((spare, *lines.shape[1:]), lines.dtype)])


def sum_in_order(parts, axes, order):
    inside = parts.shape[1:]
    parts = parts.reshape(*(lax.axis_size(a) for a in axes), *inside)
    parts = jnp.moveaxis(parts, order, range(len(axes))).reshape(-1, *inside)
    for k in order:
        parts = lax.psum_scatter(parts, axes[k], scatter_dimension=0, tiled=True)
    return parts[0]


def gather_in_order(x, axes, order):
    parts = x
    for k in order:
        parts = lax.all_gather(parts, axes[k])
    done = order[::-1]
    back = [done.index(k) for k in range(len(axes))]
    parts = parts.transpose(*back, *range(len(axes), parts.ndim))
    return parts.reshape(-1, *x.shape)


def sum_in_two_steps(x, axes, order):
    devices, lines = (lax.axis_size(axes), x.reshape(-1, *x.shape[1:][-1:]))
    parts = padded_to(lines, devices).reshape(devices, -1, *lines.shape[1:])
    own = sum_in_order(parts, axes, order)
    whole = gather_in_order(own, axes, order[::-1]).reshape(-1, *lines.shape[1:])
    return whole[: len(lines)].reshape(x.shape)


def matmul(left, right):
    return jnp.dot(left, right, precision=lax.Precision.HIGHEST, preferred_element_type=jnp.float32)


def contract(left, right, left_dim, right_dim):
    return lax.dot_general(
        left,
        right,
        (((left_dim,), (right_dim,)), ((), ())),
        precision=lax.Precision.HIGHEST,
        preferred_element_type=jnp.float32,
    )


def lower_solve(factor, rhs):
    return lax.linalg.triangular_solve(factor, rhs, left_side=True, lower=True)


def shards(trailing, panel):
    width = panel.shape[1]
    local_rows = panel.shape[0]
    local_cols = trailing.shape[1]
    ratio = lax.axis_size(COL) // lax.axis_size("row")
    panel_t = panel.T
    factor_one = jnp.linalg.cholesky(of_everyone(matmul(panel_t, panel), "row"))
    basis_t = lower_solve(factor_one, panel_t)
    upper_r = factor_one.T
    pivot_t = broadcast(basis_t[:, :width], "row", 0)
    signs = -jnp.sign(jnp.diagonal(pivot_t))
    diag_signs = jnp.diag(signs)
    leader = (lax.axis_index("row") == 0).astype(jnp.float32)
    offset_top = jnp.concatenate(
        [diag_signs, jnp.zeros((width, local_rows - width), jnp.float32)], axis=1
    )
    refl_t = basis_t - leader * offset_top
    top_t = pivot_t - diag_signs
    chol_top = jnp.linalg.cholesky(contract(top_t, top_t, 1, 1))
    inverse_low = lower_solve(chol_top, jnp.eye(width, dtype=jnp.float32))
    inverse_top = matmul(top_t.T, matmul(inverse_low.T, inverse_low))
    block_t = -signs[:, None] * inverse_top
    position = lax.axis_index(COL) % ratio * local_cols
    owner = lax.axis_index(COL) // ratio
    column_refl = broadcast(lax.dynamic_slice_in_dim(refl_t, position, local_cols, 1), "row", owner)
    partial_value = contract(column_refl, trailing, 1, 1)
    rows_x = sum_in_two_steps(partial_value, COL, (0, 1))
    cols_x = broadcast(lax.dynamic_slice_in_dim(rows_x, position, local_cols, 1), "row", owner)
    inner_sum = of_everyone(contract(refl_t, rows_x, 1, 1), "row")
    inner_scaled = matmul(inner_sum, block_t)
    coupling = matmul(block_t.T, inner_scaled)
    row_weights = matmul(block_t.T, rows_x) - 0.5 * matmul(coupling.T, refl_t)
    col_weights = matmul(block_t.T, cols_x) - 0.5 * matmul(coupling.T, column_refl)
    left_all = jnp.concatenate([refl_t, row_weights], axis=0)
    right_all = jnp.concatenate([col_weights, column_refl], axis=0)
    updated = trailing - contract(left_all, right_all, 0, 0)
    band = signs[:, None] * upper_r
    return (updated, band)


def solution(mesh):
    finer = Mesh(mesh.devices.reshape(mesh.shape["row"], 8, 4), ("row", "col_0", "col_1"))
    placed = (P("row", COL), P("row", None))
    return jax.shard_map(
        shards, mesh=finer, in_specs=placed, out_specs=(P("row", COL), P()), check_vma=False
    )
```

profile of v0, /device:TPU:1, one launch (start us, length us, event | category | flops | bytes accessed | tf_op | source)
XLA Modules:
  0.0 422.7 jit_solution(12141568029675505277)
XLA Ops:
  7.2 5.7 %fusion.63 = f32[256,256]{1,0:T(8,128)S(1)} fusion(f32[2048,256]{1,0:T(8,128)} %param.4), kind=kOutput, calls=%fused_computation.112 | convolution fusion | flops 1610612736 | bytes 2359296 | tf_op jit(solution)/shard_map/dot_general | solution.py:59
  12.9 1.5 broadcast_in_dim.40
  14.4 7.6 %all-to-all-start = ((f32[8,256,256]{2,1,0:T(8,128)}), f32[8,256,256]{2,1,0:T(8,128)}, u32[]{:S(2)}, u32[]{:S(2)}) async-start(f32[8,256,256]{2,1,0:T(8,128)} %broadcast_in_dim.40), calls=%async_computation | async-start | bytes 4194304 | tf_op jit(solution)/shard_map/all_to_all | solution.py:12
  22.4 1.8 copy.15
  24.3 24.0 %all-to-all-done = f32[8,256,256]{2,1,0:T(8,128)} async-done(((f32[8,256,256]{2,1,0:T(8,128)}), f32[8,256,256]{2,1,0:T(8,128)}, u32[]{:S(2)}, u32[]{:S(2)}) %all-to-all-start) | async-done | bytes 2097184 | tf_op jit(solution)/shard_map/all_to_all | solution.py:12
  48.2 1.8 reduce_sum.18
  50.2 11.7 %cholesky.130 = f32[128,128]{1,0:T(8,128)S(1)} custom-call(f32[128,128]{1,0:T(8,128)S(1)} %cholesky.194), custom_call_target="Cholesky" | custom-call | tf_op jit(solution)/shard_map/jit(cholesky)/cholesky | solution.py:82
  62.0 9.8 %custom-call.19 = f32[1,128,128]{1,2,0:T(8,128)S(1)} custom-call(f32[1,128,128]{2,1,0:T(8,128)S(1)} %get-tuple-element.54), custom_call_target="InvertDiagBlocksLowerTriangular" | custom-call | tf_op jit(solution)/shard_map/jit(cholesky)/cholesky | solution.py:82
  72.3 11.7 %cholesky.147 = f32[128,128]{1,0:T(8,128)S(1)} custom-call(f32[128,128]{1,0:T(8,128)S(1)} %convolution_subtract_fusion.3), custom_call_target="Cholesky" | custom-call | tf_op jit(solution)/shard_map/jit(cholesky)/cholesky | solution.py:82
  86.1 4.1 while.2
  86.8 1.3 bitcast_dynamic-update-slice_fusion.4
  88.9 1.3 bitcast_dynamic-update-slice_fusion.4
  90.2 19.8 %custom-call.14 = f32[2,128,128]{1,2,0:T(8,128)S(1)} custom-call(f32[2,128,128]{2,1,0:T(8,128)S(1)} %get-tuple-element.10), custom_call_target="InvertDiagBlocksLowerTriangular" | custom-call | tf_op jit(solution)/shard_map/triangular_solve | solution.py:73
  110.1 1.1 fusion.12
  111.2 1.9 convolution_subtract_fusion
  113.0 1.1 fusion.43
  114.1 0.8 fusion.22
  115.1 27.9 %all-gather.9.cloned.1.call-done = f32[2048,256]{1,0:T(8,128)} async-done(((f32[256,256]{1,0:T(8,128)}), f32[2048,256]{1,0:T(8,128)}) %all-gather.9.cloned.1.call-update) | async-done | bytes 2097168 | tf_op jit(solution)/shard_map/all_gather | solution.py:21
  143.0 1.0 slice.76
  144.0 2.3 gather_fusion
  147.1 1.5 fusion.10
  148.6 0.8 constant_dynamic-slice_fusion.3
  149.6 35.1 %all-gather.11.cloned.1.call-done = f32[2048,512]{1,0:T(8,128)} async-done(((f32[256,512]{1,0:T(8,128)}), f32[2048,512]{1,0:T(8,128)}) %all-gather.11.cloned.1.call-update) | async-done | bytes 4194320 | tf_op jit(solution)/shard_map/all_gather | solution.py:21
  184.7 7.3 %fusion.4 = f32[32,8,2048]{2,1,0:T(8,128)} fusion(f32[2048,512]{1,0:T(8,128)} %param.3, f32[8,256,512]{2,1,0:T(8,128)} %bitcast.110, s32[]{:T(128)S(6)} %select_n.49), kind=kOutput, calls=%fused_computation.9 | convolution fusion | flops 3221225472 | bytes 6815748 | tf_op jit(solution)/shard_map/dot_general | solution.py:63
  192.0 37.4 %reduce-scatter.3.cloned.1.call-done = f32[4,8,2048]{2,1,0:T(8,128)} async-done(((f32[32,8,2048]{2,1,0:T(8,128)}), f32[4,8,2048]{2,1,0:T(8,128)}) %reduce-scatter.3.cloned.1.call-update) | async-done | bytes 262160 | tf_op jit(solution)/shard_map/reduce_scatter | solution.py:36
  229.5 27.1 %reduce-scatter.5.cloned.1.call-done = f32[1,8,2048]{2,1,0:T(8,128)} async-done(((f32[4,8,2048]{2,1,0:T(8,128)}), f32[1,8,2048]{2,1,0:T(8,128)}) %reduce-scatter.5.cloned.1.call-update) | async-done | bytes 65552 | tf_op jit(solution)/shard_map/reduce_scatter | solution.py:36
  256.6 10.3 %all_gather.31 = f32[4,8,2048]{2,1,0:T(8,128)} all-gather(f32[1,8,2048]{2,1,0:T(8,128)} %reduce-scatter.5.cloned.1.call-done), channel_id=1, replica_groups=mesh['row'=8,'col_0'=8,'col_1'=4] {'col_1'}, dimensions={0}, use_global_device_ids=true | all-gather | bytes 327680 | tf_op jit(solution)/shard_map/all_gather | solution.py:43
  267.2 41.5 %all-gather.13.cloned.1.call-done = f32[32,8,2048]{2,1,0:T(8,128)} async-done(((f32[4,8,2048]{2,1,0:T(8,128)}), f32[32,8,2048]{2,1,0:T(8,128)}) %all-gather.13.cloned.1.call-update) | async-done | bytes 2097168 | tf_op jit(solution)/shard_map/all_gather | solution.py:43
  308.7 1.9 constant_dynamic-slice_fusion.2
  310.6 1.5 fusion.28
  312.4 11.7 %cholesky.164 = f32[128,128]{1,0:T(8,128)S(1)} custom-call(f32[128,128]{1,0:T(8,128)S(1)} %cholesky.197), custom_call_target="Cholesky" | custom-call | tf_op jit(solution)/shard_map/jit(cholesky)/cholesky | solution.py:94
  324.1 9.8 %custom-call.20 = f32[1,128,128]{1,2,0:T(8,128)S(1)} custom-call(f32[1,128,128]{2,1,0:T(8,128)S(1)} %get-tuple-element.50), custom_call_target="InvertDiagBlocksLowerTriangular" | custom-call | tf_op jit(solution)/shard_map/jit(cholesky)/cholesky | solution.py:94
  334.4 11.7 %cholesky.181 = f32[128,128]{1,0:T(8,128)S(1)} custom-call(f32[128,128]{1,0:T(8,128)S(1)} %convolution_subtract_fusion.2), custom_call_target="Cholesky" | custom-call | tf_op jit(solution)/shard_map/jit(cholesky)/cholesky | solution.py:94
  348.9 3.9 fusion.52
  352.8 1.5 broadcast_in_dim.43
  354.3 9.2 %all-to-all-start.1 = ((f32[8,256,256]{2,1,0:T(8,128)}), f32[8,256,256]{2,1,0:T(8,128)}, u32[]{:S(2)}, u32[]{:S(2)}) async-start(f32[8,256,256]{2,1,0:T(8,128)} %broadcast_in_dim.43), calls=%async_computation.3 | async-start | bytes 4194304 | tf_op jit(solution)/shard_map/all_to_all | solution.py:12
  363.5 4.0 while.3
  364.1 1.4 bitcast_dynamic-update-slice_fusion.5
  366.1 1.4 bitcast_dynamic-update-slice_fusion.5
  367.5 0.8 copy.17
  368.3 19.7 %custom-call.15 = f32[2,128,128]{1,2,0:T(8,128)S(1)} custom-call(f32[2,128,128]{2,1,0:T(8,128)S(1)} %get-tuple-element.18), custom_call_target="InvertDiagBlocksLowerTriangular" | custom-call | tf_op jit(solution)/shard_map/triangular_solve | solution.py:73
  389.5 1.6 convolution_multiply_fusion.2
  391.1 1.1 dynamic-slice_bitcast_fusion
  392.2 3.2 fusion.54
  395.4 1.8 reduce_sum.19
  398.2 4.9 %fusion.9 = f32[256,2048]{1,0:T(8,128)} fusion(f32[256,2048]{1,0:T(8,128)} %fusion.54, f32[256,256]{1,0:T(8,128)S(1)} %fusion.65, f32[256,2048]{1,0:T(8,128)S(1)} %fusion.10), kind=kOutput, calls=%fused_computation.13 | convolution fusion | flops 1611661312 | bytes 6553600 | tf_op jit(solution)/shard_map/dot_general | solution.py:59
  403.0 1.8 fusion.17
  405.5 10.2 %fusion.6 = f32[2048,512]{1,0:T(8,128)} fusion(f32[2048,512]{1,0:T(8,128)} %param.3, f32[256,2048]{1,0:T(8,128)S(1)} %copy-done.4, f32[256,2048]{1,0:T(8,128)S(1)} %fusion.10, f32[256,512]{1,0:T(8,128)S(1)} %dynamic-slice_bitcast_fusion, f32[256,512]{1,0:T(8,128)S(1)} %fusion.11), kind=kOutput, calls=%fused_computation.11 | convolution fusion | flops 6444810240 | bytes 13631488 | tf_op jit(solution)/shard_map/dot_general | solution.py:63
  (72 shorter events, 11.3 us)
Async XLA Ops:
  14.3 8.1 %copy-start = (f32[2048,256]{1,0:T(8,128)S(1)}, f32[2048,256]{1,0:T(8,128)}, u32[]{:S(2)}) copy-start(f32[2048,256]{1,0:T(8,128)} %param.4) | copy-start | bytes 6291460
  14.4 33.9 %all-to-all-start = ((f32[8,256,256]{2,1,0:T(8,128)}), f32[8,256,256]{2,1,0:T(8,128)}, u32[]{:S(2)}, u32[]{:S(2)}) async-start(f32[8,256,256]{2,1,0:T(8,128)} %broadcast_in_dim.40), calls=%async_computation | async-start | bytes 4194304 | tf_op jit(solution)/shard_map/all_to_all | solution.py:12
  21.9 121.1 %all-gather.9.cloned.1.call-start = ((), (), s32[]{:S(2)}) async-start(), calls=%async_computation.6 | async-start | bytes 2359296 | tf_op jit(solution)/shard_map/all_gather | solution.py:21
  50.0 60.1 %copy-start.3 = (f32[2048,256]{0,1:T(8,128)S(1)}, f32[2048,256]{0,1:T(8,128)}, u32[]{:S(2)}) copy-start(f32[2048,256]{0,1:T(8,128)} %copy.15) | copy-start | bytes 6291460
  90.2 19.9 %copy-start.5 = (f32[256,256]{1,0:T(8,128)}, f32[256,256]{1,0:T(8,128)S(1)}, u32[]{:S(2)}) copy-start(f32[256,256]{1,0:T(8,128)S(1)} %get-tuple-element.171) | copy-start | bytes 786436
  114.1 1.1 copy-start.2
  114.9 69.7 %all-gather.11.cloned.1.call-start = ((), (), s32[]{:S(2)}) async-start(), calls=%async_computation.7 | async-start | bytes 4718592 | tf_op jit(solution)/shard_map/all_gather | solution.py:21
  149.5 80.0 %reduce-scatter.3.cloned.1.call-start = ((), (), s32[]{:S(2)}) async-start(), calls=%async_computation.4 | async-start | bytes 2359296 | tf_op jit(solution)/shard_map/reduce_scatter | solution.py:36
  192.0 64.6 %reduce-scatter.5.cloned.1.call-start = ((), (), s32[]{:S(2)}) async-start(), calls=%async_computation.5 | async-start | bytes 327680 | tf_op jit(solution)/shard_map/reduce_scatter | solution.py:36
  229.5 79.2 %all-gather.13.cloned.1.call-start = ((), (), s32[]{:S(2)}) async-start(), calls=%async_computation.8 | async-start | bytes 2359296 | tf_op jit(solution)/shard_map/all_gather | solution.py:43
  267.0 136.1 %all-gather.15.cloned.1.call-start = ((), (), s32[]{:S(2)}) async-start(), calls=%async_computation.9 | async-start | bytes 4718592 | tf_op jit(solution)/shard_map/all_gather | solution.py:21
  354.3 13.2 %copy-start.6 = (f32[256,256]{0,1:T(8,128)S(1)}, f32[256,256]{0,1:T(8,128)}, u32[]{:S(2)}) copy-start(f32[256,256]{0,1:T(8,128)} %get-tuple-element.55) | copy-start | bytes 786436
  354.3 41.1 %all-to-all-start.1 = ((f32[8,256,256]{2,1,0:T(8,128)}), f32[8,256,256]{2,1,0:T(8,128)}, u32[]{:S(2)}, u32[]{:S(2)}) async-start(f32[8,256,256]{2,1,0:T(8,128)} %broadcast_in_dim.43), calls=%async_computation.3 | async-start | bytes 4194304 | tf_op jit(solution)/shard_map/all_to_all | solution.py:12
  388.0 4.2 copy-start.1
  403.0 2.5 copy-start.4
Sparse Core Ops, SparseCore 0:
  115.0 27.9 all-gather.8
  149.6 34.9 all-gather.10
  192.1 37.3 reduce-scatter.2
  231.8 24.7 reduce-scatter.4
  267.1 41.5 all-gather.12
  310.7 37.8 all-gather.14
where the time goes:
time: 427 us; the launch traced here: 423 us
  waiting for transfers between devices  193 us (45%)
  other arithmetic  115 us (27%)
  matrix products  48 us (11%)
  local copies, waits for them, and re-layouts  21.2 us (5%)
  starting transfers between devices  17.7 us (4%)
  between operations  17.3 us (4%)
  blocking collectives  10.3 us (2%)
    reduce_scatter x2, waiting for transfers between devices, sum_in_order(): parts = lax.psum_scatter(parts, axes[k], scatter_dimension=0, tiled=True)  64.5 us
    all_gather x3, waiting for transfers between devices, broadcast(): lax.all_gather(x, axis)  63 us
    all_gather x1, waiting for transfers between devices, gather_in_order(): parts = lax.all_gather(parts, axes[k])  41.5 us
    another operation x6, other arithmetic, lower_solve(): return lax.linalg.triangular_solve(factor, rhs, left_side=True, lower=True)  40.4 us
    another operation x7, other arithmetic, shards(): chol_top = jnp.linalg.cholesky(contract(top_t, top_t, 1, 1))  34.6 us
    another operation x6, other arithmetic, shards(): factor_one = jnp.linalg.cholesky(of_everyone(matmul(panel_t, panel), 'row'))  34 us
    all_to_all x2, waiting for transfers between devices, copy_for_each(): lax.all_to_all(jnp.broadcast_to(x[None], (devices, *x.shape)), axis, 0, 0...  24 us
    dot_general x4, matrix products, contract(): lax.dot_general(left, right, (((left_dim,), (right_dim,)), ((), ())), pre...  22.9 us
  transfers between devices with their start and end apart: 8, of which 6 were waited for; matrix products, arithmetic and copies ran while one was open for 20% of the time, Pallas kernels for 0%

commit v1 on v0

v1 whole, which is shorter than its diff:
```python
import functools

import jax
import jax.numpy as jnp
from jax import lax
from jax.experimental import pallas as pl
from jax.experimental.pallas import tpu as pltpu
from jax.sharding import Mesh
from jax.sharding import PartitionSpec as P

COL = ("z", "y")
ALL = ("row", "z", "y")
NB = 64
HIGHEST = lax.Precision.HIGHEST
HIGH = lax.Precision.HIGH


def dot(left, right, dims, precision):
    return lax.dot_general(
        left, right, (dims, ((), ())), precision=precision, preferred_element_type=jnp.float32
    )


def nn(left, right, precision=HIGHEST):
    return dot(left, right, ((1,), (0,)), precision)


def nt(left, right, precision=HIGHEST):
    return dot(left, right, ((1,), (1,)), precision)


def tn(left, right, precision=HIGHEST):
    return dot(left, right, ((0,), (0,)), precision)


def unit_eye(n):
    rows = lax.broadcasted_iota(jnp.int32, (n, n), 0)
    cols = lax.broadcasted_iota(jnp.int32, (n, n), 1)
    return (rows == cols).astype(jnp.float32)


def eliminate(block, full):
    aug = jnp.concatenate([block, unit_eye(NB)], axis=1)
    tiles = [aug[8 * i : 8 * i + 8] for i in range(NB // 8)]
    sub = lax.broadcasted_iota(jnp.int32, (8, 1), 0)
    for j in range(NB):
        t, s = divmod(j, 8)
        row = tiles[t][s : s + 1]
        scaled = row * (1.0 / row[:, j : j + 1])
        for i in range(0 if full else t, NB // 8):
            col = tiles[i][:, j : j + 1]
            if i == t:
                if full:
                    new = tiles[i] - jnp.where(sub == s, 0.0, col) * scaled
                    tiles[i] = jnp.where(sub == s, scaled, new)
                else:
                    tiles[i] = tiles[i] - jnp.where(sub > s, col, 0.0) * scaled
            else:
                tiles[i] = tiles[i] - col * scaled
    return jnp.concatenate(tiles, axis=0)


def factor_kernel(gram_ref, top_ref, band_ref, inv_ref, sign_ref, work):
    width = gram_ref.shape[0]
    work[:, :width] = gram_ref[...]
    work[:, width:] = unit_eye(width)
    for k in range(width // NB):
        lo, hi = k * NB, (k + 1) * NB
        done = eliminate(work[lo:hi, lo:hi], False)
        diag = jnp.sum(done[:, :NB] * unit_eye(NB), axis=1, keepdims=True)
        low = done[:, NB:] * lax.rsqrt(diag)
        rows = nn(low, work[lo:hi, :])
        work[lo:hi, :] = rows
        if hi < width:
            work[hi:, :] = work[hi:, :] - tn(rows[:, hi:width], rows)
    eye_r = lax.broadcasted_iota(jnp.int32, (width, width), 0)
    eye_c = lax.broadcasted_iota(jnp.int32, (width, width), 1)
    upper = jnp.where(eye_r <= eye_c, work[:, :width], 0.0)
    inv = jnp.where(eye_r >= eye_c, work[:, width:], 0.0)
    diag_q = jnp.sum(top_ref[...] * inv, axis=1, keepdims=True)
    signs = jnp.where(diag_q > 0.0, -1.0, jnp.where(diag_q < 0.0, 1.0, 0.0))
    band_ref[...] = signs * upper
    inv_ref[...] = inv
    row = jnp.sum(jnp.where(eye_r == eye_c, signs, 0.0), axis=0, keepdims=True)
    sign_ref[...] = jnp.broadcast_to(row, sign_ref.shape)


def block_kernel(top_ref, inv_ref, sign_ref, out_ref, work):
    width = top_ref.shape[0]
    work[:, :width] = unit_eye(width) - nt(inv_ref[...], top_ref[...]) * sign_ref[0:1, :]
    work[:, width:] = unit_eye(width)
    for k in range(width // NB):
        lo, hi = k * NB, (k + 1) * NB
        done = eliminate(work[lo:hi, lo:hi], True)
        rows = nn(done[:, NB:], work[lo:hi, :])
        cols = work[:, lo:hi]
        keep = lax.broadcasted_iota(jnp.int32, (width, 1), 0)
        cols = jnp.where((keep >= lo) & (keep < hi), 0.0, cols)
        work[...] = work[...] - nn(cols, rows)
        work[lo:hi, :] = rows
    out_ref[...] = work[:, width:]


def call(kernel, outs, *args):
    width = args[0].shape[0]
    return pl.pallas_call(
        kernel,
        out_shape=[jax.ShapeDtypeStruct(s, jnp.float32) for s in outs],
        scratch_shapes=[pltpu.VMEM((width, 2 * width), jnp.float32)],
        compiler_params=pltpu.CompilerParams(vmem_limit_bytes=32 * 2**20),
        cost_estimate=pl.CostEstimate(
            flops=2 * 10**9, bytes_accessed=4 * width * width * 6, transcendentals=0
        ),
    )(*args)


def exchange(x, axis):
    return lax.all_to_all(x, axis, 0, 0, tiled=True)


def to_everyone(x, axis):
    return exchange(jnp.broadcast_to(x[None], (lax.axis_size(axis), *x.shape)), axis)


def shift(x, axis, by):
    n = lax.axis_size(axis)
    return lax.ppermute(x, axis, [(i, (i + by) % n) for i in range(n)])


def shards(trailing, panel):
    width = panel.shape[1]
    local_rows = panel.shape[0]
    local_cols = trailing.shape[1]
    rows_n, z_n, y_n = (lax.axis_size(a) for a in ALL)
    row, z, y = (lax.axis_index(a) for a in ALL)
    piece = local_cols // rows_n
    thin = width // rows_n
    first = (row == 0).astype(jnp.float32)

    gram = tn(panel, panel).reshape(rows_n, thin, width)
    top = (first * panel[:width]).reshape(rows_n, thin, width)
    part = jnp.sum(exchange(jnp.concatenate([gram, top], axis=1), "row"), axis=0)
    whole = to_everyone(part, "row")
    gram = whole[:, :thin].reshape(width, width)
    top = whole[:, thin:].reshape(width, width)

    partial = tn(trailing, panel, HIGH).reshape(rows_n, piece, width)
    edge = (first * trailing[:width]).T.reshape(rows_n, piece, width)
    pieces = jnp.sum(exchange(jnp.concatenate([partial, edge], axis=1), "row"), axis=0)
    swap = [
        ((r * z_n + c) * y_n + k, (c * z_n + r) * y_n + k)
        for r in range(rows_n)
        for c in range(z_n)
        for k in range(y_n)
    ]
    mine = lax.dynamic_slice_in_dim(panel, y * local_cols, local_cols, 0)
    panel_piece = lax.ppermute(
        lax.dynamic_slice_in_dim(mine, z * piece, piece, 0), ALL, swap
    )

    band, inv, sign = call(
        factor_kernel, [(width, width), (width, width), (8, width)], gram, top
    )
    (block,) = call(block_kernel, [(width, width)], top, inv, sign)
    sign = sign[0:1]
    diag = unit_eye(width) * sign

    def reflectors(rows_of_panel, is_first, count):
        at = lax.broadcasted_iota(jnp.int32, (count, width), 0)
        to = lax.broadcasted_iota(jnp.int32, (count, width), 1)
        return nt(rows_of_panel, inv, HIGH) - jnp.where(at + is_first == to, sign, 0.0)

    far = 2 * local_rows
    x_piece = nt(pieces[:piece], inv, HIGH) - pieces[piece:] * sign
    y_piece = reflectors(
        panel_piece, jnp.where((z == 0) & (y == 0), row * piece, far), piece
    )
    x_swapped = lax.ppermute(x_piece, ALL, swap)
    x_block = to_everyone(x_swapped, "z").reshape(local_cols, width)
    y_rows = reflectors(panel, jnp.where(row == 0, 0, far), local_rows)
    y_block = lax.dynamic_slice_in_dim(y_rows, y * local_cols, local_cols, 0)

    both = to_everyone(jnp.concatenate([x_piece, y_piece], axis=0), "row")
    x_cols = both[:, :piece].reshape(local_cols, width)
    y_cols = both[:, piece:].reshape(local_cols, width)

    share = width // (rows_n * y_n)
    inner = tn(y_block, x_block).reshape(rows_n * y_n, share, width)
    inner = jnp.sum(exchange(inner, ("row", "y")), axis=0)
    inner = to_everyone(inner, ("row", "y")).reshape(width, width)
    coupling = tn(block, nn(inner, block))

    up = shift(x_block, "y", 1)
    down = shift(x_block, "y", -1)
    half = local_cols // 2
    over = jnp.concatenate([shift(up[:half], "y", 1), shift(down[half:], "y", -1)], axis=0)
    around = jnp.stack([x_block, up, over, down])
    x_rows = jnp.take(around, (y - jnp.arange(y_n)) % y_n, axis=0).reshape(local_rows, width)

    w_cols = nn(x_cols, block, HIGH) - nn(y_cols, coupling, HIGH)
    d_cols = nt(y_cols, block, HIGH)
    left = jnp.concatenate([y_rows, x_rows], axis=1)
    right = jnp.concatenate([w_cols, d_cols], axis=1)
    updated = trailing - nt(left, right, HIGH)
    return (updated, band)


def solution(mesh):
    finer = Mesh(mesh.devices.reshape(mesh.shape["row"], 8, 4), ALL)
    placed = (P("row", COL), P("row", None))
    return jax.shard_map(
        shards, mesh=finer, in_specs=placed, out_specs=(P("row", COL), P()), check_vma=False
    )
```

time: 427 us -> 204 us (0.48)
  waiting for transfers between devices: 193 us -> 30.6 us
  other arithmetic: 115 us -> 10.3 us
  Pallas kernels: 0 us -> 50.6 us
  starting transfers between devices: 17.7 us -> 47 us
  between operations: 17.3 us -> 0.9 us
  matrix products: 48 us -> 31.7 us
  local copies, waits for them, and re-layouts: 21.2 us -> 16.3 us
  blocking collectives: 10.3 us -> 14.9 us
    another operation x19 -> x2, other arithmetic: 109 us -> 2.72 us  [shards(): around = jnp.stack([x_block, up, over, down])]
    all_gather x4 -> x0, waiting for transfers between devices: 104 us -> none  [the longest x3 63 us: broadcast(): lax.all_gather(x, axis)]
    reduce_scatter x2 -> x0, waiting for transfers between devices: 64.5 us -> none  [sum_in_order(): parts = lax.psum_scatter(parts, axes[k], scatter_dimension=0, tiled=True)]
    pallas_call x0 -> x2, Pallas kernels: none -> 50.6 us  [call(): pl.pallas_call(kernel, out_shape=[jax.ShapeDtypeStruct(s, jnp.float32) fo...]
    all_to_all x2 -> x6, starting transfers between devices: 16.8 us -> 36.9 us  [exchange(): return lax.all_to_all(x, axis, 0, 0, tiled=True)]
    all_to_all x0 -> x1, blocking collectives: none -> 14.9 us  [exchange(): return lax.all_to_all(x, axis, 0, 0, tiled=True)]
    dot_general x13 -> x12, matrix products: 42.3 us -> 31.7 us  [dot(): lax.dot_general(left, right, (dims, ((), ())), precision=precision, prefe...]
    all_gather x1 -> x0, blocking collectives: 10.3 us -> none  [gather_in_order(): parts = lax.all_gather(parts, axes[k])]
  transfers between devices with their start and end apart: 8 -> 12, of which waited for: 6 -> 6; matrix products, arithmetic and copies ran while one was open for 20% -> 14% of each run, Pallas kernels for 0% -> 25%
where the time goes in v1:
time: 204 us; the launch traced here: 202 us
  Pallas kernels  50.6 us (25%)
  starting transfers between devices  47 us (23%)
  matrix products  31.7 us (16%)
  waiting for transfers between devices  30.6 us (15%)
  local copies, waits for them, and re-layouts  16.3 us (8%)
  blocking collectives  14.9 us (7%)
  other arithmetic  10.3 us (5%)
    pallas_call x2, Pallas kernels, call(): pl.pallas_call(kernel, out_shape=[jax.ShapeDtypeStruct(s, jnp.float32) fo...  50.6 us
    all_to_all x6, starting transfers between devices, exchange(): return lax.all_to_all(x, axis, 0, 0, tiled=True)  36.9 us
    dot_general x12, matrix products, dot(): lax.dot_general(left, right, (dims, ((), ())), precision=precision, prefe...  31.7 us
    all_to_all x6, waiting for transfers between devices, exchange(): return lax.all_to_all(x, axis, 0, 0, tiled=True)  20.8 us
    all_to_all x1, blocking collectives, exchange(): return lax.all_to_all(x, axis, 0, 0, tiled=True)  14.9 us
    gather x2, local copies, waits for them, and re-layouts, shards(): jnp.take(around, (y - jnp.arange(y_n)) % y_n, axis=0)  6.57 us
    ppermute x4, waiting for transfers between devices, shift(): return lax.ppermute(x, axis, [(i, (i + by) % n) for i in range(n)])  6.26 us
    ppermute x4, starting transfers between devices, shift(): return lax.ppermute(x, axis, [(i, (i + by) % n) for i in range(n)])  4.19 us
  transfers between devices with their start and end apart: 12, of which 6 were waited for; matrix products, arithmetic and copies ran while one was open for 14% of the time, Pallas kernels for 25%

profile of v1, /device:TPU:1, one launch (start us, length us, event | category | flops | bytes accessed | tf_op | source)
XLA Modules:
  0.0 202.4 jit_solution(16288969978988442655)
XLA Ops:
  0.7 5.8 %fusion.24 = f32[256,256]{1,0:T(8,128)S(1)} fusion(f32[2048,256]{1,0:T(8,128)} %param.3), kind=kOutput, calls=%fused_computation.52 | convolution fusion | flops 1610612736 | bytes 2359296 | tf_op jit(solution)/shard_map/dot_general | solution.py:19
  6.6 14.9 %all_to_all.35 = f32[8,64,256]{2,1,0:T(8,128)S(1)} all-to-all(f32[8,64,256]{2,1,0:T(8,128)S(1)} %pad_maximum_fusion.2), channel_id=1, replica_groups=mesh['row'=8,'z'=8,'y'=4] {'row'}, dimensions={0} | all-to-all | bytes 1048576 | tf_op jit(solution)/shard_map/all_to_all | solution.py:118
  21.5 0.8 broadcast_in_dim.62
  22.4 4.4 %all-to-all-start.1 = ((f32[8,64,256]{2,1,0:T(8,128)}), f32[8,64,256]{2,1,0:T(8,128)S(1)}, u32[]{:S(2)}, u32[]{:S(2)}) async-start(f32[8,64,256]{2,1,0:T(8,128)} %broadcast_in_dim.62), calls=%async_computation.1 | async-start | bytes 1048576 | tf_op jit(solution)/shard_map/all_to_all | solution.py:118
  26.8 6.5 %fusion.25 = f32[512,256]{1,0:T(8,128)} fusion(f32[2048,512]{1,0:T(8,128)} %param.2, f32[2048,256]{1,0:T(8,128)S(1)} %copy-done), kind=kOutput, calls=%fused_computation.53 | convolution fusion | flops 1610612736 | bytes 6815744 | tf_op jit(solution)/shard_map/dot_general | solution.py:19
  33.3 1.0 copy.9
  34.3 1.1 broadcast_multiply_fusion
  35.4 2.1 %pad_maximum_fusion.1 = f32[8,128,256]{2,1,0:T(8,128)} fusion(f32[8,64,256]{2,1,0:T(8,128)S(1)} %bitcast.67, f32[8,64,256]{2,1,0:T(8,128)} %bitcast.68), kind=kLoop, calls=%fused_computation.13 | loop fusion | flops 262144 | bytes 2097152 | tf_op jit(solution)/shard_map/concatenate | solution.py:149
  37.5 4.8 %all-to-all-start.2 = ((f32[8,128,256]{2,1,0:T(8,128)}), f32[8,128,256]{2,1,0:T(8,128)}, u32[]{:S(2)}, u32[]{:S(2)}) async-start(f32[8,128,256]{2,1,0:T(8,128)} %pad_maximum_fusion.1), calls=%async_computation.2 | async-start | bytes 2097152 | tf_op jit(solution)/shard_map/all_to_all | solution.py:118
  42.4 3.6 %collective-permute-start.5 = (f32[64,256]{1,0:T(8,128)S(1)}, f32[64,256]{1,0:T(8,128)S(1)}, u32[]{:S(2)}, u32[]{:S(2)}) collective-permute-start(f32[64,256]{1,0:T(8,128)S(1)} %constant_dynamic-slice_fusion), channel_id=1, source_target_pairs={{0,0},{1,1},{2,2},{3,3},{4,32},{5,33},{6,34},{7,35},{8,64},{9,65},... | collective-permute-start | bytes 196616 | tf_op jit(solution)/shard_map/ppermute | solution.py:157
  46.0 25.0 %shard_map.41 = (f32[256,256]{1,0:T(8,128)}, f32[256,256]{1,0:T(8,128)S(1)}, f32[8,256]{1,0:T(8,128)S(1)}) custom-call(f32[256,256]{1,0:T(8,128)S(1)} %bitcast.58, f32[256,256]{1,0:T(8,128)S(1)} %bitcast.56), custom_call_target="tpu_custom_call" | custom-call | flops 2000000000 | bytes 1572864 | tf_op jit(solution)/shard_map/pallas_call | solution.py:106
  71.0 1.3 reduce_sum.28
  72.3 0.3 convolution_subtract_fusion.2
  72.9 1.1 broadcast_in_dim.72
  74.0 9.9 %all-to-all-start.4 = ((f32[8,128,256]{2,1,0:T(8,128)}), f32[8,128,256]{2,1,0:T(8,128)}, u32[]{:S(2)}, u32[]{:S(2)}) async-start(f32[8,128,256]{2,1,0:T(8,128)} %broadcast_in_dim.72), calls=%async_computation.4 | async-start | bytes 2097152 | tf_op jit(solution)/shard_map/all_to_all | solution.py:118
  84.0 2.4 %collective-permute-start = (f32[64,256]{1,0:T(8,128)S(1)}, f32[64,256]{1,0:T(8,128)S(1)}, u32[]{:S(2)}, u32[]{:S(2)}) collective-permute-start(f32[64,256]{1,0:T(8,128)S(1)} %convolution_subtract_fusion.2), channel_id=1, source_target_pairs={{0,0},{1,1},{2,2},{3,3},{4,32},{5,33},{6,34},{7,35},{8,64},{9,65},... | collective-permute-start | bytes 196616 | tf_op jit(solution)/shard_map/ppermute | solution.py:178
  86.4 3.6 %collective-permute-done = f32[64,256]{1,0:T(8,128)S(1)} collective-permute-done((f32[64,256]{1,0:T(8,128)S(1)}, f32[64,256]{1,0:T(8,128)S(1)}, u32[]{:S(2)}, u32[]{:S(2)}) %collective-permute-start) | collective-permute-done | bytes 65568 | tf_op jit(solution)/shard_map/ppermute | solution.py:178
  90.0 9.0 %all-to-all-done.4 = f32[8,128,256]{2,1,0:T(8,128)} async-done(((f32[8,128,256]{2,1,0:T(8,128)}), f32[8,128,256]{2,1,0:T(8,128)}, u32[]{:S(2)}, u32[]{:S(2)}) %all-to-all-start.4) | async-done | bytes 1048608 | tf_op jit(solution)/shard_map/all_to_all | solution.py:118
  99.0 0.9 broadcast_in_dim.69
  99.8 6.0 %all-to-all-start.3 = ((f32[8,64,256]{2,1,0:T(8,128)}), f32[8,64,256]{2,1,0:T(8,128)S(1)}, u32[]{:S(2)}, u32[]{:S(2)}) async-start(f32[8,64,256]{2,1,0:T(8,128)} %broadcast_in_dim.69), calls=%async_computation.3 | async-start | bytes 1048576 | tf_op jit(solution)/shard_map/all_to_all | solution.py:118
  105.9 25.6 %shard_map.42 = f32[256,256]{1,0:T(8,128)S(1)} custom-call(f32[256,256]{1,0:T(8,128)S(1)} %bitcast.57, f32[256,256]{1,0:T(8,128)S(1)} %get-tuple-element.5.inv_ref, f32[8,256]{1,0:T(8,128)S(1)} %get-tuple-element.6.sign_ref), custom_call_target="tpu_custom_call" | custom-call | flops 2000000000 | bytes 1572864 | tf_op jit(solution)/shard_map/pallas_call | solution.py:106
  131.5 2.6 %fusion.7 = f32[2048,256]{0,1:T(8,128)} fusion(f32[256,256]{1,0:T(8,128)S(1)} %get-tuple-element.5.inv_ref, f32[2048,256]{1,0:T(8,128)S(1)} %copy-done, f32[256]{0:T(256)S(1)} %bitcast.73, s32[2048]{0:T(1024)S(1)} %iota_add_fusion), kind=kOutput, calls=%fused_computation.7 | convolution fusion | flops 806879232 | bytes 4465664 | tf_op jit(solution)/shard_map/dot_general | solution.py:19
  134.1 2.3 %fusion.22 = (f32[8,64,256]{2,1,0:T(8,128)}, f32[8,64,256]{2,1,0:T(8,128)S(1)}) fusion(f32[8,128,256]{2,1,0:T(8,128)} %all-to-all-done.4), kind=kLoop, calls=%fused_computation.50 | loop fusion | bytes 2097152 | tf_op jit(solution)/shard_map/slice | solution.py:184
  136.3 1.3 fusion.11
  137.6 7.0 %all-to-all-start.5 = ((f32[32,8,256]{2,1,0:T(8,128)}), f32[32,8,256]{2,1,0:T(8,128)}, u32[]{:S(2)}, u32[]{:S(2)}) async-start(f32[32,8,256]{2,1,0:T(8,128)} %fusion.11), calls=%async_computation.5 | async-start | bytes 524288 | tf_op jit(solution)/shard_map/all_to_all | solution.py:118
  144.6 2.2 %fusion.26 = f32[512,256]{1,0:T(8,128)} fusion(f32[512,256]{1,0:T(8,128)} %bitcast.66, f32[256,256]{1,0:T(8,128)S(1)} %shard_map.42), kind=kOutput, calls=%fused_computation.54 | convolution fusion | flops 201326592 | bytes 1310720 | tf_op jit(solution)/shard_map/dot_general | solution.py:19
  146.8 2.6 %collective-permute-start.3 = (f32[512,256]{1,0:T(8,128)S(1)}, f32[512,256]{1,0:T(8,128)}, u32[]{:S(2)}, u32[]{:S(2)}) collective-permute-start(f32[512,256]{1,0:T(8,128)S(1)} %bitcast.63), channel_id=1, source_target_pairs={{0,3},{1,0},{2,1},{3,2},{4,7},{5,4},{6,5},{7,6},{8,11},{9,8},{10,9... | collective-permute-start | bytes 1572872 | tf_op jit(solution)/shard_map/ppermute | solution.py:127
  149.4 4.1 %all-to-all-done.5 = f32[32,8,256]{2,1,0:T(8,128)} async-done(((f32[32,8,256]{2,1,0:T(8,128)}), f32[32,8,256]{2,1,0:T(8,128)}, u32[]{:S(2)}, u32[]{:S(2)}) %all-to-all-start.5) | async-done | bytes 262176 | tf_op jit(solution)/shard_map/all_to_all | solution.py:118
  153.5 1.0 reduce_sum.29
  154.4 0.7 broadcast_in_dim.73
  155.2 4.8 %all-to-all-start.6 = ((f32[32,8,256]{2,1,0:T(8,128)}), f32[32,8,256]{2,1,0:T(8,128)}, u32[]{:S(2)}, u32[]{:S(2)}) async-start(f32[32,8,256]{2,1,0:T(8,128)} %broadcast_in_dim.73), calls=%async_computation.6 | async-start | bytes 524288 | tf_op jit(solution)/shard_map/all_to_all | solution.py:118
  159.9 1.2 fusion.28
  161.2 7.7 %all-to-all-done.6 = f32[32,8,256]{2,1,0:T(8,128)} async-done(((f32[32,8,256]{2,1,0:T(8,128)}), f32[32,8,256]{2,1,0:T(8,128)}, u32[]{:S(2)}, u32[]{:S(2)}) %all-to-all-start.6) | async-done | bytes 262176 | tf_op jit(solution)/shard_map/all_to_all | solution.py:118
  168.9 1.4 fusion.14
  170.3 0.6 fusion.27
  170.9 1.0 slice.51
  171.9 0.9 collective-permute-start.4
  172.8 1.0 slice.50
  173.7 0.7 collective-permute-start.2
  174.5 1.2 convolution_subtract_fusion
  175.6 3.6 %collective-permute-done.4 = f32[256,256]{1,0:T(8,128)S(1)} collective-permute-done((f32[256,256]{1,0:T(8,128)S(1)}, f32[256,256]{1,0:T(8,128)S(1)}, u32[]{:S(2)}, u32[]{:S(2)}) %collective-permute-start.4) | collective-permute-done | bytes 262176 | tf_op jit(solution)/shard_map/ppermute | solution.py:127
  179.2 2.7 %collective-permute-done.2 = f32[256,256]{1,0:T(8,128)S(1)} collective-permute-done((f32[256,256]{1,0:T(8,128)S(1)}, f32[256,256]{1,0:T(8,128)S(1)}, u32[]{:S(2)}, u32[]{:S(2)}) %collective-permute-start.2) | collective-permute-done | bytes 262176 | tf_op jit(solution)/shard_map/ppermute | solution.py:127
  181.9 2.7 %pad_maximum_fusion = f32[4,512,256]{2,1,0:T(8,128)} fusion(f32[1,512,256]{2,1,0:T(8,128)} %bitcast.13, f32[1,512,256]{2,1,0:T(8,128)S(1)} %maximum_bitcast_fusion, f32[1,512,256]{2,1,0:T(8,128)} %bitcast.11, f32[1,512,256]{2,1,0:T(8,128)S(1)} %bitcast.65), kind=kLoop, calls=%fused_computation.8 | loop fusion | flops 1572864 | bytes 4194304 | tf_op jit(solution)/shard_map/stack | solution.py:197
  184.6 3.6 %gather_fusion = f32[4,512,256]{2,1,0:T(8,128)} fusion(f32[4,512,256]{2,1,0:T(8,128)} %pad_maximum_fusion, s32[1024]{0:T(1024)S(1)} %pad_clamp_fusion), kind=kCustom, calls=%fused_computation | custom fusion | bytes 4194320 | tf_op jit(solution)/shard_map/jit(_take)/gather | solution.py:198
  188.2 3.0 %copy.8 = f32[2048,256]{0,1:T(8,128)} copy(f32[2048,256]{1,0:T(8,128)} %bitcast.59) | data formatting | bytes 4194304 | tf_op jit(solution)/shard_map/jit(_take)/gather | solution.py:198
  191.2 1.9 broadcast_select_fusion
  193.2 0.8 copy-done.1
  194.0 8.3 %fusion.4 = f32[2048,512]{1,0:T(8,128)} fusion(f32[2048,512]{1,0:T(8,128)S(1)} %copy-done.1, f32[2048,256]{0,1:T(8,128)S(1)} %broadcast_select_fusion, f32[2048,256]{0,1:T(8,128)S(1)} %copy-done.2, f32[512,256]{1,0:T(8,128)S(1)} %copy-done.5, f32[512,256]{1,0:T(8,128)S(1)} %copy-done.4), kind=kOutput, calls=%fused_computation.5 | convolution fusion | flops 3223584768 | bytes 13631488 | tf_op jit(solution)/shard_map/dot_general | solution.py:19
  (36 shorter events, 0.6 us)
Async XLA Ops:
  0.6 5.9 %copy-start = (f32[2048,256]{1,0:T(8,128)S(1)}, f32[2048,256]{1,0:T(8,128)}, u32[]{:S(2)}) copy-start(f32[2048,256]{1,0:T(8,128)} %param.3) | copy-start | bytes 6291460
  22.4 15.1 %all-to-all-start.1 = ((f32[8,64,256]{2,1,0:T(8,128)}), f32[8,64,256]{2,1,0:T(8,128)S(1)}, u32[]{:S(2)}, u32[]{:S(2)}) async-start(f32[8,64,256]{2,1,0:T(8,128)} %broadcast_in_dim.62), calls=%async_computation.1 | async-start | bytes 1048576 | tf_op jit(solution)/shard_map/all_to_all | solution.py:118
  26.8 6.5 %slice-start = ((f32[2048,512]{1,0:T(8,128)}), f32[256,512]{1,0:T(8,128)S(1)}, s32[]{:S(2)}) async-start(f32[2048,512]{1,0:T(8,128)} %param.2), calls=%async_computation.7 | async-start | bytes 1048576 | tf_op jit(solution)/shard_map/slice | solution.py:148
  37.5 33.5 %all-to-all-start.2 = ((f32[8,128,256]{2,1,0:T(8,128)}), f32[8,128,256]{2,1,0:T(8,128)}, u32[]{:S(2)}, u32[]{:S(2)}) async-start(f32[8,128,256]{2,1,0:T(8,128)} %pad_maximum_fusion.1), calls=%async_computation.2 | async-start | bytes 2097152 | tf_op jit(solution)/shard_map/all_to_all | solution.py:118
  42.4 30.3 %collective-permute-start.5 = (f32[64,256]{1,0:T(8,128)S(1)}, f32[64,256]{1,0:T(8,128)S(1)}, u32[]{:S(2)}, u32[]{:S(2)}) collective-permute-start(f32[64,256]{1,0:T(8,128)S(1)} %constant_dynamic-slice_fusion), channel_id=1, source_target_pairs={{0,0},{1,1},{2,2},{3,3},{4,32},{5,33},{6,34},{7,35},{8,64},{9,65},... | collective-permute-start | bytes 196616 | tf_op jit(solution)/shard_map/ppermute | solution.py:157
  74.0 25.0 %all-to-all-start.4 = ((f32[8,128,256]{2,1,0:T(8,128)}), f32[8,128,256]{2,1,0:T(8,128)}, u32[]{:S(2)}, u32[]{:S(2)}) async-start(f32[8,128,256]{2,1,0:T(8,128)} %broadcast_in_dim.72), calls=%async_computation.4 | async-start | bytes 2097152 | tf_op jit(solution)/shard_map/all_to_all | solution.py:118
  84.0 6.0 %collective-permute-start = (f32[64,256]{1,0:T(8,128)S(1)}, f32[64,256]{1,0:T(8,128)S(1)}, u32[]{:S(2)}, u32[]{:S(2)}) collective-permute-start(f32[64,256]{1,0:T(8,128)S(1)} %convolution_subtract_fusion.2), channel_id=1, source_target_pairs={{0,0},{1,1},{2,2},{3,3},{4,32},{5,33},{6,34},{7,35},{8,64},{9,65},... | collective-permute-start | bytes 196616 | tf_op jit(solution)/shard_map/ppermute | solution.py:178
  99.8 36.5 %all-to-all-start.3 = ((f32[8,64,256]{2,1,0:T(8,128)}), f32[8,64,256]{2,1,0:T(8,128)S(1)}, u32[]{:S(2)}, u32[]{:S(2)}) async-start(f32[8,64,256]{2,1,0:T(8,128)} %broadcast_in_dim.69), calls=%async_computation.3 | async-start | bytes 1048576 | tf_op jit(solution)/shard_map/all_to_all | solution.py:118
  134.1 2.3 %copy-start.2 = (f32[2048,256]{0,1:T(8,128)S(1)}, f32[2048,256]{0,1:T(8,128)}, u32[]{:S(2)}) copy-start(f32[2048,256]{0,1:T(8,128)} %fusion.7) | copy-start | bytes 6291460
  137.6 15.8 %all-to-all-start.5 = ((f32[32,8,256]{2,1,0:T(8,128)}), f32[32,8,256]{2,1,0:T(8,128)}, u32[]{:S(2)}, u32[]{:S(2)}) async-start(f32[32,8,256]{2,1,0:T(8,128)} %fusion.11), calls=%async_computation.5 | async-start | bytes 524288 | tf_op jit(solution)/shard_map/all_to_all | solution.py:118
  146.8 24.0 %collective-permute-start.3 = (f32[512,256]{1,0:T(8,128)S(1)}, f32[512,256]{1,0:T(8,128)}, u32[]{:S(2)}, u32[]{:S(2)}) collective-permute-start(f32[512,256]{1,0:T(8,128)S(1)} %bitcast.63), channel_id=1, source_target_pairs={{0,3},{1,0},{2,1},{3,2},{4,7},{5,4},{6,5},{7,6},{8,11},{9,8},{10,9... | collective-permute-start | bytes 1572872 | tf_op jit(solution)/shard_map/ppermute | solution.py:127
  149.4 23.4 %collective-permute-start.1 = (f32[512,256]{1,0:T(8,128)S(1)}, f32[512,256]{1,0:T(8,128)}, u32[]{:S(2)}, u32[]{:S(2)}) collective-permute-start(f32[512,256]{1,0:T(8,128)S(1)} %bitcast.64), channel_id=1, source_target_pairs={{0,1},{1,2},{2,3},{3,0},{4,5},{5,6},{6,7},{7,4},{8,9},{9,10},{10,1... | collective-permute-start | bytes 1572872 | tf_op jit(solution)/shard_map/ppermute | solution.py:127
  155.2 13.7 %all-to-all-start.6 = ((f32[32,8,256]{2,1,0:T(8,128)}), f32[32,8,256]{2,1,0:T(8,128)}, u32[]{:S(2)}, u32[]{:S(2)}) async-start(f32[32,8,256]{2,1,0:T(8,128)} %broadcast_in_dim.73), calls=%async_computation.6 | async-start | bytes 524288 | tf_op jit(solution)/shard_map/all_to_all | solution.py:118
  168.9 5.6 %copy-start.3 = (f32[512,256]{1,0:T(8,128)S(1)}, f32[512,256]{1,0:T(8,128)}, u32[]{:S(2)}) copy-start(f32[512,256]{1,0:T(8,128)} %fusion.26) | copy-start | bytes 1572868
  171.9 7.4 %collective-permute-start.4 = (f32[256,256]{1,0:T(8,128)S(1)}, f32[256,256]{1,0:T(8,128)S(1)}, u32[]{:S(2)}, u32[]{:S(2)}) collective-permute-start(f32[256,256]{1,0:T(8,128)S(1)} %slice.51), channel_id=1, source_target_pairs={{0,3},{1,0},{2,1},{3,2},{4,7},{5,4},{6,5},{7,6},{8,11},{9,8},{10,9... | collective-permute-start | bytes 786440 | tf_op jit(solution)/shard_map/ppermute | solution.py:127
  173.7 8.1 %collective-permute-start.2 = (f32[256,256]{1,0:T(8,128)S(1)}, f32[256,256]{1,0:T(8,128)S(1)}, u32[]{:S(2)}, u32[]{:S(2)}) collective-permute-start(f32[256,256]{1,0:T(8,128)S(1)} %slice.50), channel_id=1, source_target_pairs={{0,1},{1,2},{2,3},{3,0},{4,5},{5,6},{6,7},{7,4},{8,9},{9,10},{10,1... | collective-permute-start | bytes 786440 | tf_op jit(solution)/shard_map/ppermute | solution.py:127
  188.2 4.9 %copy-start.4 = (f32[512,256]{1,0:T(8,128)S(1)}, f32[512,256]{1,0:T(8,128)}, u32[]{:S(2)}) copy-start(f32[512,256]{1,0:T(8,128)} %convolution_subtract_fusion) | copy-start | bytes 1572868
  188.2 4.9 %copy-start.5 = (f32[512,256]{1,0:T(8,128)S(1)}, f32[512,256]{1,0:T(8,128)}, u32[]{:S(2)}) copy-start(f32[512,256]{1,0:T(8,128)} %fusion.28) | copy-start | bytes 1572868
  191.2 2.8 %copy-start.1 = (f32[2048,512]{1,0:T(8,128)S(1)}, f32[2048,512]{1,0:T(8,128)}, u32[]{:S(2)}) copy-start(f32[2048,512]{1,0:T(8,128)} %param.2) | copy-start | bytes 12582916
